TPU v7x, 32 devices: a whole 2x2x4 slice. The times are simulated.
32 devices in a mesh: kpt: 2 (over y), ga: 16 (over z, x, core).
Axes of the slice: x: 2, y: 2, z: 4, core: 2. Of those that a mesh axis runs over, the one named last changes fastest.
Arguments:
- miller_index: int32 [3, 12288], P(None, 'ga'), may hold values from -12 to 12
- kpoint: float32 [6], P('kpt'), parts along dimension 0, may hold values from -0.5 to 0.5
- waves: bfloat16 [2, 256, 12288], P(None, 'kpt', 'ga'), parts along dimension 1, may hold values from -6 to 6
- species: int32 [16], replicated, may hold values from 0 to 3
- counts: int32 [16], replicated, may hold values from 1 to 8
- positions: int32 [3, 16], replicated, may hold values from 0 to 63
- radial_coef: float32 [4, 8, 16], replicated, may hold values from -4 to 4
- coupling: float32 [16, 8, 8], replicated, as said below
Outputs:
- applied: bfloat16 [2, 256, 12288], P(None, 'kpt', 'ga'), parts along dimension 1
- energy: float32 [256], P('kpt'), parts along dimension 0
There are 2 independent parts, one for each index of `kpt`. A program takes and returns all parts, laid end to end along the dimension named above; an argument that names none is the same for every part. Nothing has to cross between parts.
Inputs may be any that keep to these rules, and one draw needn't show every extreme that they name: `coupling`: symmetric in its last two dimensions.
All inputs are finite; a program needn't handle non-finite values.
Results may differ from a plain program's by a relative error of at most 0.0062.
Values may be sent and summed in bfloat16 or wider, within the bound.
A program may use at most 64 MiB of HBM per device.

v0:
```python
import math
import jax
import jax.numpy as jnp
from jax import lax
from jax.sharding import PartitionSpec as P

PROJ = 8
MGRID = 64
ATOM_BLOCK = 16


def prepare(miller_index, kpoint, terms):
    shifted = miller_index.astype(jnp.float32) + kpoint[:, None]
    squared = jnp.sum(shifted * shifted, axis=0)
    widths = 0.001 * 1.5 ** jnp.arange(terms).astype(jnp.float32)
    basis = jnp.exp(-widths[:, None] * squared[None, :])
    angular = jnp.concatenate(
        [jnp.ones_like(squared)[None], shifted / jnp.sqrt(squared + 1.0)[None]], 0
    )
    angular = jnp.concatenate([angular, angular], 0)
    return (basis, angular)


def projectors(
    first, miller_index, kpoint, basis, angular, species, counts, positions, radial_coef, scaling
):
    kinds = lax.dynamic_slice_in_dim(species, first, ATOM_BLOCK)
    numbers = lax.dynamic_slice_in_dim(counts, first, ATOM_BLOCK)
    places = lax.dynamic_slice_in_dim(positions, first, ATOM_BLOCK, 1)
    selector = (kinds[:, None] == jnp.arange(radial_coef.shape[0])[None, :]).astype(jnp.float32)
    chosen = jnp.einsum("as,sjr->ajr", selector, radial_coef, precision=lax.Precision.HIGHEST)
    radial = jnp.einsum("ajr,rg->ajg", chosen, basis, precision=lax.Precision.HIGHEST)
    active = (jnp.arange(PROJ)[None, :] < numbers[:, None]).astype(jnp.float32)
    amplitude = radial * angular[None] * active[:, :, None] * scaling
    winding = jnp.mod(jnp.sum(miller_index[:, None, :] * places[:, :, None], axis=0), MGRID)
    offset = jnp.sum(kpoint[:, None] * places.astype(jnp.float32), axis=0)
    phase = 2.0 * math.pi / MGRID * (winding.astype(jnp.float32) + offset[:, None])
    planes = miller_index.shape[1]
    real_part = (
        (amplitude * jnp.cos(phase)[:, None, :])
        .astype(jnp.bfloat16)
        .reshape(ATOM_BLOCK * PROJ, planes)
    )
    imag_part = (
        (-amplitude * jnp.sin(phase)[:, None, :])
        .astype(jnp.bfloat16)
        .reshape(ATOM_BLOCK * PROJ, planes)
    )
    return (real_part, imag_part)


def measure(real_part, imag_part, coeffs):
    over_re = jnp.einsum(
        "sg,bg->sb", real_part, coeffs[0], preferred_element_type=jnp.float32
    ) + jnp.einsum("sg,bg->sb", imag_part, coeffs[1], preferred_element_type=jnp.float32)
    over_im = jnp.einsum(
        "sg,bg->sb", real_part, coeffs[1], preferred_element_type=jnp.float32
    ) - jnp.einsum("sg,bg->sb", imag_part, coeffs[0], preferred_element_type=jnp.float32)
    return jnp.stack([over_re, over_im])


def spread(rows, real_part, imag_part):
    out_re = jnp.einsum(
        "sb,sg->bg", rows[0], real_part, preferred_element_type=jnp.float32
    ) - jnp.einsum("sb,sg->bg", rows[1], imag_part, preferred_element_type=jnp.float32)
    out_im = jnp.einsum(
        "sb,sg->bg", rows[1], real_part, preferred_element_type=jnp.float32
    ) + jnp.einsum("sb,sg->bg", rows[0], imag_part, preferred_element_type=jnp.float32)
    return jnp.stack([out_re, out_im])


def on_device(miller_index, kpoint, waves, species, counts, positions, radial_coef, coupling):
    planes = waves.shape[2]
    bands = waves.shape[1]
    scaling = 1.0 / math.sqrt(planes * lax.axis_size("ga"))
    atoms = coupling.shape[0]
    slots_all = atoms * PROJ
    blocks = atoms // ATOM_BLOCK
    width = ATOM_BLOCK * PROJ
    basis, angular = prepare(miller_index, kpoint, radial_coef.shape[2])

    def build(index):
        return projectors(
            index * ATOM_BLOCK,
            miller_index,
            kpoint,
            basis,
            angular,
            species,
            counts,
            positions,
            radial_coef,
            scaling,
        )

    empty = jnp.zeros((2, bands, planes), jnp.float32)

    def first_pass(index, table):
        real_part, imag_part = build(index)
        return lax.dynamic_update_slice_in_dim(
            table, measure(real_part, imag_part, waves), index * width, 1
        )

    local = lax.fori_loop(0, blocks, first_pass, jnp.zeros((2, slots_all, bands), jnp.float32))
    summed = lax.psum(local, "ga")
    shaped = summed.reshape(2, atoms, PROJ, summed.shape[2])
    weighted = jnp.einsum("aij,cajb->caib", coupling, shaped, precision=lax.Precision.HIGHEST)
    weighted = weighted.reshape(2, atoms * PROJ, summed.shape[2])
    energy = jnp.sum(summed * weighted, axis=(0, 1))
    table = weighted.astype(jnp.bfloat16)

    def second_pass(index, output):
        real_part, imag_part = build(index)
        rows = lax.dynamic_slice_in_dim(table, index * width, width, 1)
        return output + spread(rows, real_part, imag_part)

    output = lax.fori_loop(0, blocks, second_pass, empty)
    return (output.astype(jnp.bfloat16), energy / slots_all)


def solution(mesh):
    in_specs = (P(None, "ga"), P("kpt"), P(None, "kpt", "ga"), P(), P(), P(), P(), P())
    out_specs = (P(None, "kpt", "ga"), P("kpt"))
    return jax.shard_map(
        on_device, mesh=mesh, in_specs=in_specs, out_specs=out_specs, check_vma=False
    )
```

profile of v0, /device:TPU:8, one launch (start us, length us, event | category | flops | bytes accessed | tf_op | source)
XLA Modules:
  0.0 116.9 jit_solution(3049479459820801523)
XLA Ops:
  7.2 0.0 copy-start
  7.2 0.0 all-reduce.2.cloned.1.call-start
  7.3 0.6 copy-done.6
  7.8 0.8 multiply_reduce_fusion.2
  8.6 0.8 multiply_reduce_fusion.1
  9.4 0.1 multiply_reduce_fusion
  9.5 0.1 fusion.35
  9.6 0.6 copy-done.8
  10.2 0.1 fusion.38
  10.3 0.3 fusion.40
  10.6 0.4 copy-done.7
  10.9 0.2 fusion.33
  11.2 0.6 fusion.8
  11.8 0.4 copy-done.1
  12.2 0.2 fusion.9
  12.4 0.2 fusion.13
  12.6 0.2 fusion.5
  12.8 0.2 fusion.6
  13.1 0.7 pad_maximum_fusion.1
  13.7 0.0 all-reduce.2.cloned.1.call-update
  13.8 0.7 copy-done.4
  14.5 0.1 copy.18
  14.6 91.3 %all-reduce.2.cloned.1.call-done = f32[2,128,128]{2,1,0:T(8,128)} async-done(((f32[2,128,128]{2,1,0:T(8,128)}), f32[2,128,128]{2,1,0:T(8,128)}) %all-reduce.2.cloned.1.call-update) | async-done | bytes 131088 | tf_op jit(solution)/shard_map/psum | solution.py:105
  105.9 1.1 convolution_bitcast_fusion
  107.1 0.2 fusion.30
  107.3 0.2 fusion.29
  107.6 0.7 copy-done.2
  108.2 0.1 fusion.19
  108.3 0.5 broadcast_multiply_fusion
  108.8 0.2 fusion.3
  109.1 0.2 fusion.4
  109.3 0.8 pad_maximum_fusion
  (16 shorter events, 0.1 us)
Async XLA Ops:
  7.2 3.4 %copy-start = (f32[4,8,16]{2,1,0:T(8,128)S(1)}, f32[4,8,16]{2,1,0:T(8,128)}, u32[]{:S(2)}) copy-start(f32[4,8,16]{2,1,0:T(8,128)} %param.14) | copy-start | bytes 6148
  7.2 0.7 copy-start.6
  7.2 2.2 %copy-start.3 = (s32[3,768]{1,0:T(4,128)S(1)}, s32[3,768]{1,0:T(4,128)}, u32[]{:S(2)}) copy-start(s32[3,768]{1,0:T(4,128)} %param.8) | copy-start | bytes 27652
  7.2 98.7 %all-reduce.2.cloned.1.call-start = ((), (), s32[]{:S(2)}) async-start(), calls=%async_computation | async-start | bytes 262144 | tf_op jit(solution)/shard_map/psum | solution.py:105
  8.6 0.8 copy-start.5
  9.5 0.7 copy-start.8
  10.3 0.7 copy-start.7
  11.2 1.0 copy-start.1
  13.7 0.8 copy-start.4
  107.3 0.9 copy-start.2
Sparse Core Ops, SparseCore 0:
  13.9 92.0 all-reduce.1
where the time goes:
time: 117 us
  waiting for transfers between devices  91.4 us (78%)
  between operations  14.2 us (12%)
  other arithmetic  4.1 us (4%)
  matrix products  3.75 us (3%)
  local copies, waits for them, and re-layouts  3.45 us (3%)
    psum x1, waiting for transfers between devices, on_device(): summed = lax.psum(local, 'ga')  91.3 us
    unnamed x19, local copies, waits for them, and re-layouts  3.43 us
  transfers between devices with their start and end apart: 1, of which 1 were waited for; matrix products, arithmetic and copies ran while one was open for 0% of the time, Pallas kernels for 0%

commit v1 on v0

--- a/solution.py
+++ b/solution.py
@@ -102,7 +102,7 @@
         )
 
     local = lax.fori_loop(0, blocks, first_pass, jnp.zeros((2, slots_all, bands), jnp.float32))
-    summed = lax.psum(local, "ga")
+    summed = jnp.sum(lax.all_gather(local, "ga"), axis=0)
     shaped = summed.reshape(2, atoms, PROJ, summed.shape[2])
     weighted = jnp.einsum("aij,cajb->caib", coupling, shaped, precision=lax.Precision.HIGHEST)
     weighted = weighted.reshape(2, atoms * PROJ, summed.shape[2])

time: 117 us -> 72.3 us (0.62)
  the two profiles are of different devices: /device:TPU:8 before, /device:TPU:0 now
where the time goes in v1:
time: 72.3 us; the launch traced here: 71.9 us
  waiting for transfers between devices  44.2 us (61%)
  between operations  14.2 us (20%)
  other arithmetic  7.88 us (11%)
  matrix products  5.4 us (7%)
    all_gather x1, waiting for transfers between devices, on_device(): summed = jnp.sum(lax.all_gather(local, 'ga'), axis=0)  44.2 us
    reduce_sum x1, other arithmetic, on_device(): summed = jnp.sum(lax.all_gather(local, 'ga'), axis=0)  1.7 us
  transfers between devices with their start and end apart: 1, of which 1 were waited for; matrix products, arithmetic and copies ran while one was open for 0% of the time, Pallas kernels for 0%

profile of v1, /device:TPU:0, one launch (start us, length us, event | category | flops | bytes accessed | tf_op | source)
XLA Modules:
  0.0 71.9 jit_solution(4743672532773135019)
XLA Ops:
  7.2 0.0 copy-start
  7.2 0.0 copy-start.1
  7.2 0.0 copy-start.2
  7.2 0.0 all-gather.3.cloned.1.call-start
  7.2 0.8 %multiply_reduce_fusion = s32[16,768]{1,0:T(8,128)S(1)} fusion(s32[3,16]{1,0:T(4,128)} %param.13, s32[3,768]{1,0:T(4,128)} %param.8), kind=kLoop, calls=%fused_computation.28 | loop fusion | flops 61440 | bytes 58560 | tf_op jit(solution)/shard_map/while/body/eval_jaxpr/reduce_sum | solution.py:35
  8.1 0.8 %multiply_reduce_fusion.3 = f32[16]{0:T(128)S(1)} fusion(s32[3,16]{1,0:T(4,128)} %param.13, f32[3]{0:T(128)} %param.9), kind=kLoop, calls=%fused_computation.59 | loop fusion | flops 128 | bytes 268 | tf_op jit(solution)/shard_map/while/body/eval_jaxpr/reduce_sum | solution.py:36
  8.9 0.8 %multiply_reduce_fusion.2 = f32[768]{0:T(1024)S(1)} fusion(s32[3,768]{1,0:T(4,128)} %param.8, f32[3]{0:T(128)} %param.9), kind=kLoop, calls=%fused_computation.53 | loop fusion | flops 8448 | bytes 12300 | tf_op jit(solution)/shard_map/reduce_sum | solution.py:14
  9.7 0.8 %fusion.34 = f32[3,768]{1,0:T(4,128)S(1)} fusion(s32[3,768]{1,0:T(4,128)} %param.8, f32[768]{0:T(1024)S(1)} %add_sqrt_fusion, f32[3]{0:T(128)} %param.9), kind=kLoop, calls=%fused_computation.55 | loop fusion | flops 6912 | bytes 21516 | tf_op jit(solution)/shard_map/div | solution.py:18
  10.5 0.7 %fusion.35 = f32[16,8]{1,0:T(8,128)S(1)} fusion(s32[16]{0:T(128)} %param.12), kind=kLoop, calls=%fused_computation.57 | loop fusion | flops 256 | bytes 576 | tf_op jit(solution)/shard_map/while/body/eval_jaxpr/convert_element_type | solution.py:33
  11.2 0.3 fusion.39
  11.5 0.0 copy-done
  11.5 0.9 %fusion.32 = f32[16,8,16]{2,0,1:T(8,128)S(1)} fusion(f32[4,8,16]{2,1,0:T(8,128)S(1)} %copy-done, s32[16]{0:T(128)} %param.11), kind=kOutput, calls=%fused_computation.51 | convolution fusion | flops 98368 | bytes 10304 | tf_op jit(solution)/shard_map/while/body/eval_jaxpr/as,sjr->ajr/dot_general | solution.py:31
  12.4 0.6 fusion.8
  13.0 1.1 %fusion.13 = f32[128,128]{1,0:T(8,128)S(1)} fusion(bf16[128,768]{1,0:T(8,128)(2,1)S(1)} %get-tuple-element.51, bf16[2,128,768]{2,1,0:T(8,128)(2,1)} %param.10), kind=kOutput, calls=%fused_computation.22 | convolution fusion | flops 25165824 | bytes 458752 | tf_op jit(solution)/shard_map/while/body/eval_jaxpr/sg,bg->sb/dot_general | solution.py:53
  14.1 1.1 %fusion.9 = f32[128,128]{1,0:T(8,128)S(1)} fusion(bf16[128,768]{1,0:T(8,128)(2,1)S(1)} %get-tuple-element.51, bf16[2,128,768]{2,1,0:T(8,128)(2,1)} %param.10), kind=kOutput, calls=%fused_computation.18 | convolution fusion | flops 25165824 | bytes 458752 | tf_op jit(solution)/shard_map/while/body/eval_jaxpr/sg,bg->sb/dot_general | solution.py:56
  15.3 0.0 copy-done.1
  15.3 0.2 fusion.6
  15.5 0.2 fusion.5
  15.7 0.7 pad_maximum_fusion.1
  16.4 0.0 all-gather.3.cloned.1.call-update
  16.4 0.0 copy-done.2
  16.4 0.1 copy.24
  16.5 44.2 %all-gather.3.cloned.1.call-done = f32[32,128,128]{2,1,0:T(8,128)} async-done(((f32[2,128,128]{2,1,0:T(8,128)}), f32[32,128,128]{2,1,0:T(8,128)}) %all-gather.3.cloned.1.call-update) | async-done | bytes 2097168 | tf_op jit(solution)/shard_map/all_gather | solution.py:105
  60.8 1.7 %reduce_sum.60 = f32[2,128,128]{2,1,0:T(8,128)S(1)} reduce(f32[16,2,128,128]{3,2,1,0:T(8,128)} %bitcast.56, f32[]{:T(128)} %constant.62.clone.1), dimensions={0}, to_apply=%region_3.4 | reduce | flops 491520 | bytes 2228228 | tf_op jit(solution)/shard_map/reduce_sum | solution.py:105
  62.5 0.3 multiply_reduce_fusion.1
  62.7 0.2 fusion.28
  63.0 0.2 fusion.29
  63.2 0.2 fusion.4
  63.5 0.2 fusion.3
  63.7 0.5 broadcast_multiply_fusion
  64.2 0.8 %pad_maximum_fusion = bf16[2,128,768]{2,1,0:T(8,128)(2,1)} fusion(bf16[1,128,768]{2,1,0:T(8,128)(2,1)S(1)} %fusion.3, bf16[1,128,768]{2,1,0:T(8,128)(2,1)S(1)} %fusion.4), kind=kLoop, calls=%fused_computation.13 | loop fusion | flops 196608 | bytes 786432 | tf_op jit(solution)/shard_map/while/body/eval_jaxpr/stack | solution.py:69
  (4 shorter events, 0.0 us)
Async XLA Ops:
  7.2 4.3 %copy-start = (f32[4,8,16]{2,1,0:T(8,128)S(1)}, f32[4,8,16]{2,1,0:T(8,128)}, u32[]{:S(2)}) copy-start(f32[4,8,16]{2,1,0:T(8,128)} %param.14) | copy-start | bytes 6148
  7.2 8.1 %copy-start.1 = (bf16[2,128,768]{2,1,0:T(8,128)(2,1)S(1)}, bf16[2,128,768]{2,1,0:T(8,128)(2,1)}, u32[]{:S(2)}) copy-start(bf16[2,128,768]{2,1,0:T(8,128)(2,1)} %param.10) | copy-start | bytes 1179652
  7.2 9.2 %copy-start.2 = (f32[16,8,8]{0,2,1:T(8,128)S(1)}, f32[16,8,8]{0,2,1:T(8,128)}, u32[]{:S(2)}) copy-start(f32[16,8,8]{0,2,1:T(8,128)} %param.15) | copy-start | bytes 12292
  7.2 53.6 %all-gather.3.cloned.1.call-start = ((), (), s32[]{:S(2)}) async-start(), calls=%async_computation | async-start | bytes 2228224 | tf_op jit(solution)/shard_map/all_gather | solution.py:105
Sparse Core Ops, SparseCore 0:
  16.5 44.1 all-gather.2
